TPU v7x, 32 devices: a whole 2x2x4 slice. The times are simulated.
32 devices in a mesh: run: 2 (over y), gx: 4 (over x, core), gy: 4 (over z).
Axes of the slice: x: 2, y: 2, z: 4, core: 2. Of those that a mesh axis runs over, the one named last changes fastest.
Arguments:
- magnet: float32 [3, 4, 256, 256], P(None, None, ('run', 'gx', 'gy')), parts along dimension 2, may hold values from -1 to 1, as said below
- window_shift: int32 [2], P('run'), parts along dimension 0, may hold values from 1 to 7
- region: int32 [256, 256], P(('run', 'gx', 'gy')), parts along dimension 0, may hold values 0 or 1
- material: float32 [4, 5], replicated, may hold values from 0.1 to 1
- kernel: float32 [6, 7, 256, 256], P(None, None, ('gx', 'gy')), may hold values from -6 to 6, as said below
Outputs:
- magnet_next: float32 [3, 4, 256, 256], P(None, None, ('run', 'gx', 'gy')), parts along dimension 2
- effective_field: float32 [3, 4, 256, 256], P(None, None, ('run', 'gx', 'gy')), parts along dimension 2
There are 2 independent parts, one for each index of `run`. A program takes and returns all parts, laid end to end along the dimension named above; an argument that names none is the same for every part. Nothing has to cross between parts.
Inputs may be any that keep to these rules, and one draw needn't show every extreme that they name: `magnet`: each cell's three components form a unit vector. kernel[c, d, ky, kx] equals t_c kernel[c, d, ky, (256 - kx) mod 256] with t_c = -1 for c = 3 and 4, 1 otherwise; it equals u_c kernel[c, 6 - d, ky, kx] with u_c = -1 for c = 4 and 5, 1 otherwise; components 3 and 5 are zero at ky = 0.
All inputs are finite; a program needn't handle non-finite values. No bound on the sum of `region` on one device may be relied on, other than what follows from the above.
Results may differ from a plain program's by a relative error of at most 0.0001.
Values sent between devices are 32-bit elements; how exact they have to be, the bound alone decides.
A program may use at most 128 MiB of HBM per device.

v0:
```python
import functools
import math

import jax
import jax.numpy as jnp
import numpy as np
from jax import lax
from jax.experimental import pallas as pl
from jax.experimental.pallas import tpu as pltpu
from jax.sharding import PartitionSpec as P

time_step = 0.1
pair_comp = ((0, 3, 4), (3, 1, 5), (4, 5, 2))
lane_tile = 128
f32, bf16 = jnp.float32, jnp.bfloat16


def split_table(table):
    high = table.astype(bf16)
    low = (table - high.astype(np.float64)).astype(bf16)
    return np.stack([high, low])


def width_tables(width, devices, track_freq):
    length = 2 * width - 1
    angle = 2.0 * math.pi / length * (np.arange(width)[:, None] * np.arange(width)[None, :] % length)
    both = np.stack([np.cos(angle), -np.sin(angle)], axis=1)
    both = both.reshape(width, 2, devices, width // devices).transpose(0, 2, 1, 3)
    forward = both.reshape(width, 2 * width)
    weight = np.where(np.arange(width) == 0, 1.0, 2.0).reshape(devices, 1, width // devices)
    inverse = (both * weight).reshape(width, 2 * width).T / (2.0 * track_freq * length)
    return split_table(forward), split_table(inverse)


def track_tables(cells):
    freq = 2 * cells
    angle = 2.0 * math.pi / freq * (np.arange(cells)[:, None] * np.arange(cells)[None, :] % freq)
    cosine, sine = np.cos(angle), np.sin(angle)
    sine[:, 0] = np.where(np.arange(cells) % 2 == 0, 1.0, -1.0)
    forward = np.concatenate([cosine, sine], axis=1)
    weight = np.where(np.arange(freq) % cells == 0, 1.0, 2.0)[:, None]
    return split_table(forward), split_table(forward.T * weight)


def product(values, table):
    rows = values.shape[0]
    high = values.astype(bf16)
    low = (values - high.astype(f32)).astype(bf16)
    first = jnp.dot(jnp.concatenate([high, low], axis=0), table[0], preferred_element_type=f32)
    second = jnp.dot(high, table[1], preferred_element_type=f32)
    return first[:rows] + first[rows:] + second


def turned(power, parts):
    real, imag = parts
    return ((real, imag), (-imag, real), (-real, -imag), (imag, -real))[power % 4]


def kernel_body(
    grid_y, devices, layers,
    shift_ref, material_ref, magnet_ref, region_ref, *refs,
):
    hbm_refs, (next_ref, field_ref), loaded, load_sems, shift_cell, rest = (
        refs[:5], refs[5:7], refs[7:12], refs[12], refs[13], refs[14:]
    )
    kernel_ref, fwd_y, inv_y, fwd_t, inv_t = loaded
    loads = [
        pltpu.make_async_copy(source, target, load_sems.at[n])
        for n, (source, target) in enumerate(zip((*hbm_refs, shift_ref), (*loaded, shift_cell)))
    ]
    for load in loads[1:2] + loads[:1] + loads[2:]:
        load.start()
    run_step(
        grid_y, devices, layers, loads, shift_cell, material_ref, magnet_ref, region_ref,
        kernel_ref, fwd_y, inv_y, fwd_t, inv_t, next_ref, field_ref, *rest,
    )


def run_step(
    grid_y, devices, layers, loads,
    shift_ref, material_ref, magnet_ref, region_ref, kernel_ref, fwd_y, inv_y, fwd_t, inv_t,
    next_ref, field_ref,
    joined, initial, state, local_field, slope_ref, halo_out, halo_in, spec, table,
    send_a, recv_a, send_b, recv_b, track_hat, track_prod,
    fill_ref, win_sem, halo_sems, a_send_sem, a_recv_sem, b_send_sem, b_recv_sem,
):
    fields, rows, width = state.shape
    half = layers // 2
    freqs = kernel_ref.shape[2]
    track = devices * rows
    block = 2 * freqs
    groups, _, _, padded = send_a.shape
    group_fields = fields // groups
    group_rows = group_fields * block
    me = lax.axis_index("gx") * grid_y + lax.axis_index("gy")

    def device_of(peer):
        return {"gx": peer // grid_y, "gy": lax.rem(peer, grid_y)}

    def peer_at(offset):
        return lax.rem(me + offset, devices)

    right, left = peer_at(1), peer_at(devices - 1)
    grid_x = devices // grid_y
    my_x, my_y = lax.axis_index("gx"), lax.axis_index("gy")
    others = []
    for k in range(grid_y - 1):
        high, low = grid_y - 1 - k, k
        far_y = jnp.where(
            my_y < grid_y // 2,
            high - jnp.where(my_y >= high, 1, 0),
            low + jnp.where(my_y <= low, 1, 0),
        )
        others += [(lax.rem(my_x + a, grid_x), far_y) for a in range(grid_x)]
    others += [(lax.rem(my_x + a, grid_x), my_y) for a in range(1, grid_x)]

    others = others[::-1]
    barrier = pltpu.get_barrier_semaphore()
    for offset in range(1, devices):
        pl.semaphore_signal(barrier, inc=1, device_id=device_of(peer_at(offset)))

    lane_small = lax.broadcasted_iota(jnp.int32, (rows, lane_tile), 1)

    def place(c, sign, z):
        return ((sign ^ (c == 2)) * 3 + c) * half + z

    tiles_all = padded // lane_tile
    cut_a = -(-3 * half * block // lane_tile)
    cut_b = 3 * half * block // lane_tile
    parts_a = [part for part in ((0, cut_a), (cut_a, tiles_all)) if part[0] < part[1]]
    parts_b = [part for part in ((0, cut_b), (cut_b, tiles_all)) if part[0] < part[1]]

    def lanes(part):
        return pl.ds(part[0] * lane_tile, (part[1] - part[0]) * lane_tile)

    def in_block(start):
        return (lane_small >= start) & (lane_small < start + block)

    def halo_copies():
        return [
            pltpu.make_async_remote_copy(
                src_ref=halo_out.at[side], dst_ref=halo_in.at[1 - side],
                send_sem=halo_sems.at[0, side], recv_sem=halo_sems.at[1, 1 - side],
                device_id=device_of(peer),
            )
            for side, peer in ((0, left), (1, right))
        ]

    def exchange(source, target, send_sem, recv_sem, parts, n, other):
        peer = other[0] * grid_y + other[1]
        return pltpu.make_async_remote_copy(
            src_ref=source.at[0, peer, :, lanes(parts[n])],
            dst_ref=target.at[0, me, :, lanes(parts[n])],
            send_sem=send_sem.at[n], recv_sem=recv_sem.at[n],
            device_id={"gx": other[0], "gy": other[1]},
        )

    def all_blocks(source, target, send_sem, recv_sem, parts, n):
        others = pl.ds(0, devices - 1)
        return pltpu.make_async_remote_copy(
            src_ref=source.at[0, others, :, lanes(parts[n])],
            dst_ref=target.at[0, others, :, lanes(parts[n])],
            send_sem=send_sem.at[n], recv_sem=recv_sem.at[n],
            device_id=device_of(right),
        )

    a_refs = (send_a, recv_a, a_send_sem, a_recv_sem, parts_a)
    b_refs = (send_b, recv_b, b_send_sem, b_recv_sem, parts_b)

    def width_blocks(values, target):
        for group in range(groups):
            spec[...] = product(
                jnp.concatenate(
                    values[group * group_fields : (group + 1) * group_fields], axis=0
                ),
                fwd_y,
            )
            for d in range(devices):
                tile, start = divmod(d * block, lane_tile)
                tiles = [jnp.zeros((rows, lane_tile), f32)] * (padded // lane_tile)
                for f in range(group_fields):
                    to_tile, to_start = divmod(f * block, lane_tile)
                    piece = spec[pl.ds(f * rows, rows), pl.ds(tile * lane_tile, lane_tile)]
                    if to_start != start:
                        piece = pltpu.roll(piece, (to_start - start) % lane_tile, 1)
                    tiles[to_tile] = jnp.where(in_block(to_start), piece, tiles[to_tile])
                for t, value in enumerate(tiles):
                    target[group, d, :, pl.ds(t * lane_tile, lane_tile)] = value

    def mirrored(cells):
        values = [None] * fields
        for c in range(3):
            for z in range(half):
                a, b = cells[c * layers + z], cells[c * layers + layers - 1 - z]
                values[place(c, 0, z)] = a + b
                values[place(c, 1, z)] = a - b
        return values

    def send_forward():
        for n in range(len(parts_a)):
            for o in others:
                exchange(*a_refs, n, o).start()
        recv_a[0, me] = send_a[0, me]

    loads[1].wait()
    width_blocks(mirrored(magnet_ref), send_a)
    pl.semaphore_wait(barrier, devices - 1)
    send_forward()
    window_copy = pltpu.make_async_remote_copy(
        src_ref=magnet_ref, dst_ref=joined.at[:, pl.ds(rows, rows)],
        send_sem=win_sem.at[0], recv_sem=win_sem.at[1], device_id=device_of(left),
    )
    window_copy.start()

    joined[:, pl.ds(0, rows)] = magnet_ref[...]
    fill_values = [
        jnp.full((rows, width), 2.0 if f // half == 5 else 0.0, f32) for f in range(fields)
    ]
    width_blocks(fill_values, send_b)
    fill_ref[...] = send_b[:, me]
    loads[0].wait()
    lane_track = lax.broadcasted_iota(jnp.int32, (freqs, track), 1)
    for c in range(6):
        for z in range(half):
            for w in range(half):
                near = kernel_ref[c, layers - 1 + z - w]
                far = kernel_ref[c, 2 * layers - 2 - z - w]
                for sign, value in enumerate((near + far, near - far)):
                    cosines = value[:, :track]
                    table[c, z, w, sign, :, pl.ds(0, track)] = cosines
                    table[c, z, w, sign, :, pl.ds(track, track)] = jnp.where(
                        lane_track == 0, value[:, track:], cosines
                    )
    if padded > group_rows:
        track_prod[...] = jnp.zeros_like(track_prod)
    for load in loads[2:]:
        load.wait()
    window_copy.wait()

    offset = shift_ref[0]
    row_index = lax.broadcasted_iota(jnp.int32, (rows, width), 0)
    lane_index = lax.broadcasted_iota(jnp.int32, (rows, width), 1)
    beyond = track - offset
    for f in range(fields):
        fill = 1.0 if f // layers == 2 else 0.0
        moved = pltpu.roll(joined[f], 2 * rows - offset, 0)
        cells = jnp.where(me * rows + row_index >= beyond, fill, moved[:rows])
        initial[f] = cells
        state[f] = cells
        next_ref[f] = cells
        halo_in[0, pl.ds(f, 1), :] = jnp.where(
            me * rows - 1 >= beyond, fill, moved[2 * rows - 1 :]
        )
        halo_in[1, pl.ds(f, 1), :] = jnp.where(
            me * rows + rows >= beyond, fill, moved[rows : rows + 1]
        )

    def stage(step, carry):
        @pl.when(step > 0)
        def _():
            for copy in halo_copies():
                copy.wait()

        flow = region_ref[...].astype(f32)
        for z in range(layers):
            drift = material_ref[z, 4] * flow
            for c in range(3):
                f = c * layers + z
                cells = state[f]
                before = jnp.where(me == 0, cells[0:1], halo_in[0, pl.ds(f, 1), :])
                after = jnp.where(
                    me == devices - 1, cells[rows - 1 : rows], halo_in[1, pl.ds(f, 1), :]
                )
                up = jnp.where(row_index == 0, before, pltpu.roll(cells, 1, 0))
                down = jnp.where(row_index == rows - 1, after, pltpu.roll(cells, rows - 1, 0))
                side_a = jnp.where(lane_index == 0, cells, pltpu.roll(cells, 1, 1))
                side_b = jnp.where(
                    lane_index == width - 1, cells, pltpu.roll(cells, width - 1, 1)
                )
                below = state[c * layers + max(z - 1, 0)]
                above = state[c * layers + min(z + 1, layers - 1)]
                laplace = up + down + side_a + side_b + below + above - 6.0 * cells
                effective = material_ref[z, 2] * laplace
                if c == 2:
                    effective = effective + material_ref[z, 3] * cells
                local_field[f] = effective
                slope_ref[f] = drift * (0.5 * (down - up))

        def arrive(n):
            all_blocks(*a_refs, n).wait_recv()
            part = lanes(parts_a[n])

            @pl.when(step == 0)
            def _():
                whole = recv_a[0, :, :, part].reshape(track, part.size)
                moved = pltpu.roll(whole, track - offset, 0)
                cell = lax.broadcasted_iota(jnp.int32, moved.shape, 0)
                moved = jnp.where(cell >= beyond, fill_ref[0, pl.ds(0, 1), part], moved)
                recv_a[0, :, :, part] = moved.reshape(devices, rows, part.size)

            arrived = recv_a[0, :, :, part].reshape(track, part.size)
            track_hat[part] = product(arrived.T, fwd_t)

        def give_back(n):
            part = lanes(parts_b[n])
            back = product(track_prod[part], inv_t).T
            send_b[0, :, :, part] = back.reshape(devices, rows, part.size)
            for o in others:
                exchange(*b_refs, n, o).start()
            recv_b[0, me, :, part] = send_b[0, me, :, part]

        def hat(c, sign, z, odd):
            first = place(c, sign, z) * block
            return tuple(
                track_hat[pl.ds(first + p * freqs, freqs), pl.ds(odd * track, track)]
                for p in range(2)
            )

        for chosen in range(2):
            if chosen < len(parts_a):
                arrive(chosen)
            for i in range(3):
                sign = chosen ^ (i == 2)
                for z in range(half):
                    for odd in range(2):
                        total = [None, None]
                        for j in range(3):
                            c = pair_comp[i][j]
                            power = 1 if c >= 4 else 0
                            swap = c in (3, 4)
                            if swap:
                                power += 1 if odd else 3
                            for w in range(half):
                                tab = table[c, z, w, sign, :, pl.ds(odd * track, track)]
                                source = hat(
                                    j, sign ^ (c >= 4), w, 1 - odd if swap else odd
                                )
                                parts = turned(power, tuple(tab * value for value in source))
                                total = [
                                    part if old is None else old + part
                                    for old, part in zip(total, parts)
                                ]
                        first = place(i, sign, z) * block
                        for p in range(2):
                            track_prod[
                                pl.ds(first + p * freqs, freqs), pl.ds(odd * track, track)
                            ] = total[p]

            if chosen == 1 or len(parts_b) == 2:
                give_back(min(chosen, len(parts_b) - 1))

        demag = []
        for group in range(groups):
            for f in range(group_fields):
                from_tile, from_start = divmod(f * block, lane_tile)
                for n, part in enumerate(parts_b):
                    if from_start == 0 and from_tile == part[0]:
                        all_blocks(*b_refs, n).wait_recv()
                tiles = [None] * (2 * width // lane_tile)
                for d in range(devices):
                    tile, start = divmod(d * block, lane_tile)
                    piece = recv_b[group, d, :, pl.ds(from_tile * lane_tile, lane_tile)]
                    if from_start != start:
                        piece = pltpu.roll(piece, (start - from_start) % lane_tile, 1)
                    old = tiles[tile]
                    tiles[tile] = piece if old is None else jnp.where(in_block(start), piece, old)
                for t, value in enumerate(tiles):
                    spec[pl.ds(f * rows, rows), pl.ds(t * lane_tile, lane_tile)] = value
            field = product(spec[...], inv_y)
            demag += [field[f * rows : (f + 1) * rows] for f in range(group_fields)]

        weight = jnp.where((step == 0) | (step == 3), time_step / 6.0, time_step / 3.0)
        ahead = jnp.where(step == 2, time_step, 0.5 * time_step)

        def demag_of(c, sign, z):
            return demag[place(c, sign, z)]

        for z in range(layers):
            mirror = min(z, layers - 1 - z)
            m, h, g = [], [], []
            for c in range(3):
                f = c * layers + z
                even, odd = demag_of(c, 0, mirror), demag_of(c, 1, mirror)
                value = local_field[f] + (even + odd if z < half else even - odd)

                @pl.when(step == 0)
                def _():
                    field_ref[f] = value

                m.append(state[f])
                h.append(value)
                g.append(slope_ref[f])

            def cross(a, b):
                return [
                    a[1] * b[2] - a[2] * b[1],
                    a[2] * b[0] - a[0] * b[2],
                    a[0] * b[1] - a[1] * b[0],
                ]

            damping = jnp.full((rows, width), material_ref[z, 0], f32)
            adiabatic = material_ref[z, 1]
            scale = 1.0 / (1.0 + damping * damping)
            torque_h, torque_u = cross(m, h), cross(m, g)
            inner = [
                (1.0 + damping * adiabatic) * u - damping * t for t, u in zip(torque_h, torque_u)
            ]
            outer = cross(m, inner)
            for c in range(3):
                f = c * layers + z
                change = (outer[c] - torque_h[c] + (adiabatic - damping) * torque_u[c]) * scale
                next_ref[f] = next_ref[f] + weight * change
                state[f] = initial[f] + ahead * change

        for refs in (a_refs, b_refs):
            for n in range(len(refs[-1])):
                all_blocks(*refs, n).wait_send()

        @pl.when(step < 3)
        def _():
            for f in range(fields):
                halo_out[0, pl.ds(f, 1), :] = state[f, pl.ds(0, 1), :]
                halo_out[1, pl.ds(f, 1), :] = state[f, pl.ds(rows - 1, 1), :]
            for copy in halo_copies():
                copy.start()
            width_blocks(mirrored(state), send_a)
            send_forward()

        return carry

    lax.fori_loop(0, 4, stage, 0)


def local(magnet, window_shift, region, material, kernel):
    components, layers, rows, width = magnet.shape
    grid_y = lax.axis_size("gy")
    devices = lax.axis_size("gx") * grid_y
    fields = components * layers
    track = rows * devices
    freqs = kernel.shape[2]
    groups = 1
    padded = -(-fields // groups * 2 * freqs // lane_tile) * lane_tile
    tables = (*width_tables(width, devices, 2 * track), *track_tables(track))
    vmem = pl.BlockSpec(memory_space=pltpu.VMEM)
    smem = pl.BlockSpec(memory_space=pltpu.SMEM)
    cells = (fields, rows, width)
    half = layers // 2
    blocks = (groups, devices, rows, padded)
    out = jax.ShapeDtypeStruct(cells, f32)
    dma = pltpu.SemaphoreType.DMA
    magnet_next, field = pl.pallas_call(
        functools.partial(kernel_body, grid_y, devices, layers),
        out_shape=(out, out),
        in_specs=[pl.BlockSpec(memory_space=pl.ANY), smem, vmem, vmem] + [pl.BlockSpec(memory_space=pl.ANY)] * 5,
        out_specs=(vmem, vmem),
        scratch_shapes=[
            pltpu.VMEM(kernel.shape, f32),
            *[pltpu.VMEM(table.shape, bf16) for table in tables],
            dma((6,)),
            pltpu.SMEM((1,), jnp.int32),
            pltpu.VMEM((fields, 2 * rows, width), f32),
            pltpu.VMEM(cells, f32),
            pltpu.VMEM(cells, f32),
            pltpu.VMEM(cells, f32),
            pltpu.VMEM(cells, f32),
            pltpu.VMEM((2, fields, width), f32),
            pltpu.VMEM((2, fields, width), f32),
            pltpu.VMEM((fields // groups * rows, 2 * width), f32),
            pltpu.VMEM((6, half, half, 2, freqs, 2 * track), f32),
            pltpu.VMEM(blocks, f32),
            pltpu.VMEM(blocks, f32),
            pltpu.VMEM(blocks, f32),
            pltpu.VMEM(blocks, f32),
            pltpu.VMEM((groups * padded, 2 * track), f32),
            pltpu.VMEM((groups * padded, 2 * track), f32),
            pltpu.VMEM((groups, rows, padded), f32),
            dma((2,)),
            dma((2, 2)),
            dma((2,)),
            dma((2,)),
            dma((2,)),
            dma((2,)),
        ],
        compiler_params=pltpu.CompilerParams(
            collective_id=0, has_side_effects=True, vmem_limit_bytes=60 * 2**20
        ),
    )(
        window_shift,
        material,
        magnet.reshape(cells),
        region,
        kernel,
        *[jnp.asarray(table) for table in tables],
    )
    return magnet_next.reshape(magnet.shape), field.reshape(magnet.shape)


def solution(mesh):
    cells = P(None, None, ("run", "gx", "gy"), None)
    in_specs = (
        cells,
        P("run"),
        P(("run", "gx", "gy"), None),
        P(),
        P(None, None, ("gx", "gy"), None),
    )
    return jax.shard_map(
        local, mesh=mesh, in_specs=in_specs, out_specs=(cells, cells), check_vma=False
    )
```

profile of v0, /device:TPU:0, one launch (start us, length us, event | category | flops | bytes accessed | tf_op | source)
XLA Modules:
  0.0 68.4 jit_solution(408589422131558929)
XLA Ops:
  1.3 64.9 %shard_map.104 = (f32[12,8,256]{2,1,0:T(8,128)}, f32[12,8,256]{2,1,0:T(8,128)}) custom-call(s32[1]{0:T(128)S(6)} %copy.13.shift_ref, f32[4,5]{1,0:T(4,128)} %material_ref.1, f32[12,8,256]{2,1,0:T(8,128)} %bitcast.3, s32[8,256]{1,0:T(8,128)} %region_ref.1, f32[6,7,16,256]{3,2,1,0:T(8,128)} %refs_0_.1, bf16[2,256,512]{2,1,0:T(8,128)(2,1)} %constant.8.clone.refs_1_, ...), custom_call_target="tpu_custom_call" | custom-call | tf_op jit(solution)/shard_map/pallas_call | solution.py:451
  66.2 0.0 copy-start
  66.2 1.6 %copy.14 = f32[3,4,8,256]{3,2,1,0:T(8,128)} copy(f32[3,4,8,256]{3,2,1,0:T(8,128)} %bitcast.5) | data formatting | bytes 196608
  67.7 0.0 copy-done
  67.7 0.6 copy.15
Async XLA Ops:
  66.2 1.6 %copy-start = (f32[12,8,256]{2,1,0:T(8,128)S(1)}, f32[12,8,256]{2,1,0:T(8,128)}, u32[]{:S(2)}) copy-start(f32[12,8,256]{2,1,0:T(8,128)} %get-tuple-element.5) | copy-start | bytes 294916
where the time goes:
time: 68.6 us; the launch traced here: 68.4 us
  Pallas kernels  64.9 us (95%)
  local copies, waits for them, and re-layouts  2.22 us (3%)
  between operations  1.29 us (2%)
    pallas_call x1, Pallas kernels, local(): pl.pallas_call(functools.partial(kernel_body, grid_y, devices, layers), o...  64.9 us
    unnamed x4, local copies, waits for them, and re-layouts  2.22 us

commit v1 on v0

--- a/solution.py
+++ b/solution.py
@@ -58,17 +58,17 @@
 
 def kernel_body(
     grid_y, devices, layers,
-    shift_ref, material_ref, magnet_ref, region_ref, *refs,
+    *refs,
 ):
-    hbm_refs, (next_ref, field_ref), loaded, load_sems, shift_cell, rest = (
-        refs[:5], refs[5:7], refs[7:12], refs[12], refs[13], refs[14:]
+    hbm_refs, shift_cell, (next_ref, field_ref), loaded, load_sems, rest = (
+        refs[:8], refs[8], refs[9:11], refs[11:19], refs[19], refs[20:]
     )
-    kernel_ref, fwd_y, inv_y, fwd_t, inv_t = loaded
+    magnet_ref, fwd_y, kernel_ref, inv_y, fwd_t, inv_t, material_ref, region_ref = loaded
     loads = [
         pltpu.make_async_copy(source, target, load_sems.at[n])
-        for n, (source, target) in enumerate(zip((*hbm_refs, shift_ref), (*loaded, shift_cell)))
+        for n, (source, target) in enumerate(zip(hbm_refs, loaded))
     ]
-    for load in loads[1:2] + loads[:1] + loads[2:]:
+    for load in loads:
         load.start()
     run_step(
         grid_y, devices, layers, loads, shift_cell, material_ref, magnet_ref, region_ref,
@@ -136,11 +136,12 @@
     def in_block(start):
         return (lane_small >= start) & (lane_small < start + block)
 
-    def halo_copies():
+    def halo_copies(step):
         return [
             pltpu.make_async_remote_copy(
-                src_ref=halo_out.at[side], dst_ref=halo_in.at[1 - side],
-                send_sem=halo_sems.at[0, side], recv_sem=halo_sems.at[1, 1 - side],
+                src_ref=halo_out.at[side], dst_ref=halo_in.at[lax.rem(step, 2), 1 - side],
+                send_sem=halo_sems.at[lax.rem(step, 2), 0, side],
+                recv_sem=halo_sems.at[lax.rem(step, 2), 1, 1 - side],
                 device_id=device_of(peer),
             )
             for side, peer in ((0, left), (1, right))
@@ -202,7 +203,8 @@
                 exchange(*a_refs, n, o).start()
         recv_a[0, me] = send_a[0, me]
 
-    loads[1].wait()
+    for load in loads[:2]:
+        load.wait()
     width_blocks(mirrored(magnet_ref), send_a)
     pl.semaphore_wait(barrier, devices - 1)
     send_forward()
@@ -218,7 +220,8 @@
     ]
     width_blocks(fill_values, send_b)
     fill_ref[...] = send_b[:, me]
-    loads[0].wait()
+    for load in loads[2:]:
+        load.wait()
     lane_track = lax.broadcasted_iota(jnp.int32, (freqs, track), 1)
     for c in range(6):
         for z in range(half):
@@ -233,59 +236,29 @@
                     )
     if padded > group_rows:
         track_prod[...] = jnp.zeros_like(track_prod)
-    for load in loads[2:]:
-        load.wait()
-    window_copy.wait()
 
     offset = shift_ref[0]
     row_index = lax.broadcasted_iota(jnp.int32, (rows, width), 0)
     lane_index = lax.broadcasted_iota(jnp.int32, (rows, width), 1)
     beyond = track - offset
-    for f in range(fields):
-        fill = 1.0 if f // layers == 2 else 0.0
-        moved = pltpu.roll(joined[f], 2 * rows - offset, 0)
-        cells = jnp.where(me * rows + row_index >= beyond, fill, moved[:rows])
-        initial[f] = cells
-        state[f] = cells
-        next_ref[f] = cells
-        halo_in[0, pl.ds(f, 1), :] = jnp.where(
-            me * rows - 1 >= beyond, fill, moved[2 * rows - 1 :]
-        )
-        halo_in[1, pl.ds(f, 1), :] = jnp.where(
-            me * rows + rows >= beyond, fill, moved[rows : rows + 1]
-        )
+
+    def set_window():
+        window_copy.wait()
+        for f in range(fields):
+            fill = 1.0 if f // layers == 2 else 0.0
+            moved = pltpu.roll(joined[f], 2 * rows - offset, 0)
+            cells = jnp.where(me * rows + row_index >= beyond, fill, moved[:rows])
+            initial[f] = cells
+            state[f] = cells
+            next_ref[f] = cells
+            halo_in[0, 0, pl.ds(f, 1), :] = jnp.where(
+                me * rows - 1 >= beyond, fill, moved[2 * rows - 1 :]
+            )
+            halo_in[0, 1, pl.ds(f, 1), :] = jnp.where(
+                me * rows + rows >= beyond, fill, moved[rows : rows + 1]
+            )
 
     def stage(step, carry):
-        @pl.when(step > 0)
-        def _():
-            for copy in halo_copies():
-                copy.wait()
-
-        flow = region_ref[...].astype(f32)
-        for z in range(layers):
-            drift = material_ref[z, 4] * flow
-            for c in range(3):
-                f = c * layers + z
-                cells = state[f]
-                before = jnp.where(me == 0, cells[0:1], halo_in[0, pl.ds(f, 1), :])
-                after = jnp.where(
-                    me == devices - 1, cells[rows - 1 : rows], halo_in[1, pl.ds(f, 1), :]
-                )
-                up = jnp.where(row_index == 0, before, pltpu.roll(cells, 1, 0))
-                down = jnp.where(row_index == rows - 1, after, pltpu.roll(cells, rows - 1, 0))
-                side_a = jnp.where(lane_index == 0, cells, pltpu.roll(cells, 1, 1))
-                side_b = jnp.where(
-                    lane_index == width - 1, cells, pltpu.roll(cells, width - 1, 1)
-                )
-                below = state[c * layers + max(z - 1, 0)]
-                above = state[c * layers + min(z + 1, layers - 1)]
-                laplace = up + down + side_a + side_b + below + above - 6.0 * cells
-                effective = material_ref[z, 2] * laplace
-                if c == 2:
-                    effective = effective + material_ref[z, 3] * cells
-                local_field[f] = effective
-                slope_ref[f] = drift * (0.5 * (down - up))
-
         def arrive(n):
             all_blocks(*a_refs, n).wait_recv()
             part = lanes(parts_a[n])
@@ -349,6 +322,42 @@
             if chosen == 1 or len(parts_b) == 2:
                 give_back(min(chosen, len(parts_b) - 1))
 
+        @pl.when(step == 0)
+        def _():
+            set_window()
+
+        @pl.when(step > 0)
+        def _():
+            for copy in halo_copies(step):
+                copy.wait()
+
+        turn = lax.rem(step, 2)
+
+        flow = region_ref[...].astype(f32)
+        for z in range(layers):
+            drift = material_ref[z, 4] * flow
+            for c in range(3):
+                f = c * layers + z
+                cells = state[f]
+                before = jnp.where(me == 0, cells[0:1], halo_in[turn, 0, pl.ds(f, 1), :])
+                after = jnp.where(
+                    me == devices - 1, cells[rows - 1 : rows], halo_in[turn, 1, pl.ds(f, 1), :]
+                )
+                up = jnp.where(row_index == 0, before, pltpu.roll(cells, 1, 0))
+                down = jnp.where(row_index == rows - 1, after, pltpu.roll(cells, rows - 1, 0))
+                side_a = jnp.where(lane_index == 0, cells, pltpu.roll(cells, 1, 1))
+                side_b = jnp.where(
+                    lane_index == width - 1, cells, pltpu.roll(cells, width - 1, 1)
+                )
+                below = state[c * layers + max(z - 1, 0)]
+                above = state[c * layers + min(z + 1, layers - 1)]
+                laplace = up + down + side_a + side_b + below + above - 6.0 * cells
+                effective = material_ref[z, 2] * laplace
+                if c == 2:
+                    effective = effective + material_ref[z, 3] * cells
+                local_field[f] = effective
+                slope_ref[f] = drift * (0.5 * (down - up))
+
         demag = []
         for group in range(groups):
             for f in range(group_fields):
@@ -418,13 +427,13 @@
 
         @pl.when(step < 3)
         def _():
+            width_blocks(mirrored(state), send_a)
+            send_forward()
             for f in range(fields):
                 halo_out[0, pl.ds(f, 1), :] = state[f, pl.ds(0, 1), :]
                 halo_out[1, pl.ds(f, 1), :] = state[f, pl.ds(rows - 1, 1), :]
-            for copy in halo_copies():
+            for copy in halo_copies(step + 1):
                 copy.start()
-            width_blocks(mirrored(state), send_a)
-            send_forward()
 
         return carry
 
@@ -442,29 +451,31 @@
     padded = -(-fields // groups * 2 * freqs // lane_tile) * lane_tile
     tables = (*width_tables(width, devices, 2 * track), *track_tables(track))
     vmem = pl.BlockSpec(memory_space=pltpu.VMEM)
-    smem = pl.BlockSpec(memory_space=pltpu.SMEM)
     cells = (fields, rows, width)
     half = layers // 2
     blocks = (groups, devices, rows, padded)
-    out = jax.ShapeDtypeStruct(cells, f32)
+    out = pltpu.VMEM(cells, f32)
     dma = pltpu.SemaphoreType.DMA
     magnet_next, field = pl.pallas_call(
         functools.partial(kernel_body, grid_y, devices, layers),
         out_shape=(out, out),
-        in_specs=[pl.BlockSpec(memory_space=pl.ANY), smem, vmem, vmem] + [pl.BlockSpec(memory_space=pl.ANY)] * 5,
+        in_specs=[pl.BlockSpec(memory_space=pltpu.HBM)] * 8 + [pl.BlockSpec(memory_space=pltpu.SMEM)],
         out_specs=(vmem, vmem),
         scratch_shapes=[
+            pltpu.VMEM(cells, f32),
+            pltpu.VMEM(tables[0].shape, bf16),
             pltpu.VMEM(kernel.shape, f32),
-            *[pltpu.VMEM(table.shape, bf16) for table in tables],
-            dma((6,)),
-            pltpu.SMEM((1,), jnp.int32),
+            *[pltpu.VMEM(table.shape, bf16) for table in tables[1:]],
+            pltpu.SMEM(material.shape, f32),
+            pltpu.VMEM(region.shape, jnp.int32),
+            dma((8,)),
             pltpu.VMEM((fields, 2 * rows, width), f32),
             pltpu.VMEM(cells, f32),
             pltpu.VMEM(cells, f32),
             pltpu.VMEM(cells, f32),
             pltpu.VMEM(cells, f32),
             pltpu.VMEM((2, fields, width), f32),
-            pltpu.VMEM((2, fields, width), f32),
+            pltpu.VMEM((2, 2, fields, width), f32),
             pltpu.VMEM((fields // groups * rows, 2 * width), f32),
             pltpu.VMEM((6, half, half, 2, freqs, 2 * track), f32),
             pltpu.VMEM(blocks, f32),
@@ -475,7 +486,7 @@
             pltpu.VMEM((groups * padded, 2 * track), f32),
             pltpu.VMEM((groups, rows, padded), f32),
             dma((2,)),
-            dma((2, 2)),
+            dma((2, 2, 2)),
             dma((2,)),
             dma((2,)),
             dma((2,)),
@@ -485,12 +496,13 @@
             collective_id=0, has_side_effects=True, vmem_limit_bytes=60 * 2**20
         ),
     )(
+        magnet.reshape(cells),
+        jnp.asarray(tables[0]),
+        kernel,
+        *[jnp.asarray(table) for table in tables[1:]],
+        material,
+        region,
         window_shift,
-        material,
-        magnet.reshape(cells),
-        region,
-        kernel,
-        *[jnp.asarray(table) for table in tables],
     )
     return magnet_next.reshape(magnet.shape), field.reshape(magnet.shape)
 

time: 68.6 us -> 64.5 us (0.940)
  Pallas kernels: 64.9 us -> 61.8 us
  local copies, waits for them, and re-layouts: 2.22 us -> 1.28 us
    pallas_call x1, Pallas kernels: 64.9 us -> 61.8 us  [local(): pl.pallas_call(functools.partial(kernel_body, grid_y, devices, layers), o...]
    unnamed x4 -> x2, local copies, waits for them, and re-layouts: 2.22 us -> 1.28 us
where the time goes in v1:
time: 64.5 us; the launch traced here: 64.4 us
  Pallas kernels  61.8 us (96%)
  local copies, waits for them, and re-layouts  1.28 us (2%)
  between operations  1.28 us (2%)
    pallas_call x1, Pallas kernels, local(): pl.pallas_call(functools.partial(kernel_body, grid_y, devices, layers), o...  61.8 us

profile of v1, /device:TPU:0, one launch (start us, length us, event | category | flops | bytes accessed | tf_op | source)
XLA Modules:
  0.0 64.4 jit_solution(11994442308204894481)
XLA Ops:
  1.3 61.8 %shard_map.104 = (f32[12,8,256]{2,1,0:T(8,128)S(1)}, f32[12,8,256]{2,1,0:T(8,128)S(1)}) custom-call(f32[12,8,256]{2,1,0:T(8,128)} %bitcast.5, bf16[2,256,512]{2,1,0:T(8,128)(2,1)} %constant.8.clone.refs_1_, f32[6,7,16,256]{3,2,1,0:T(8,128)} %refs_2_.1, bf16[2,512,256]{2,1,0:T(8,128)(2,1)} %constant.9.clone.refs_3_, ...), custom_call_target="tpu_custom_call" | custom-call | tf_op jit(solution)/shard_map/pallas_call | solution.py:459
  63.1 0.6 copy.13
  63.7 0.6 copy.14

commit v2 on v1

--- a/solution.py
+++ b/solution.py
@@ -18,7 +18,11 @@
 def split_table(table):
     high = table.astype(bf16)
     low = (table - high.astype(np.float64)).astype(bf16)
-    return np.stack([high, low])
+    return np.concatenate([high, low], axis=1)
+
+
+def deep(table):
+    return np.concatenate([table, table], axis=0)
 
 
 def width_tables(width, devices, track_freq):
@@ -39,15 +43,25 @@
     sine[:, 0] = np.where(np.arange(cells) % 2 == 0, 1.0, -1.0)
     forward = np.concatenate([cosine, sine], axis=1)
     weight = np.where(np.arange(freq) % cells == 0, 1.0, 2.0)[:, None]
-    return split_table(forward), split_table(forward.T * weight)
+    tables = split_table(forward), split_table(forward.T * weight)
+    return tuple(deep(table) for table in tables) if cells <= lane_tile else tables
 
 
 def product(values, table):
-    rows = values.shape[0]
+    depth, columns = values.shape[1], table.shape[1] // 2
     high = values.astype(bf16)
     low = (values - high.astype(f32)).astype(bf16)
-    first = jnp.dot(jnp.concatenate([high, low], axis=0), table[0], preferred_element_type=f32)
-    second = jnp.dot(high, table[1], preferred_element_type=f32)
+    if table.shape[0] > depth:
+        both = jnp.concatenate([high, low], axis=1)
+        out = jnp.dot(both, table[...], preferred_element_type=f32)
+        return out[:, :columns] + out[:, columns:]
+    rows = values.shape[0]
+    both = jnp.concatenate([high, low], axis=0)
+    if columns <= 2 * lane_tile:
+        out = jnp.dot(both, table[...], preferred_element_type=f32)
+        return out[:rows, :columns] + (out[rows:, :columns] + out[:rows, columns:])
+    first = jnp.dot(both, table[:, :columns], preferred_element_type=f32)
+    second = jnp.dot(high, table[:, columns:], preferred_element_type=f32)
     return first[:rows] + first[rows:] + second
 
 
@@ -60,16 +74,15 @@
     grid_y, devices, layers,
     *refs,
 ):
-    hbm_refs, shift_cell, (next_ref, field_ref), loaded, load_sems, rest = (
-        refs[:8], refs[8], refs[9:11], refs[11:19], refs[19], refs[20:]
+    hbm_refs, shift_cell, out_ref, loaded, load_sems, rest = (
+        refs[:8], refs[8], refs[9], refs[10:18], refs[18], refs[19:]
     )
+    next_ref, field_ref = out_ref.at[0], out_ref.at[1]
     magnet_ref, fwd_y, kernel_ref, inv_y, fwd_t, inv_t, material_ref, region_ref = loaded
     loads = [
         pltpu.make_async_copy(source, target, load_sems.at[n])
         for n, (source, target) in enumerate(zip(hbm_refs, loaded))
     ]
-    for load in loads:
-        load.start()
     run_step(
         grid_y, devices, layers, loads, shift_cell, material_ref, magnet_ref, region_ref,
         kernel_ref, fwd_y, inv_y, fwd_t, inv_t, next_ref, field_ref, *rest,
@@ -103,21 +116,19 @@
     right, left = peer_at(1), peer_at(devices - 1)
     grid_x = devices // grid_y
     my_x, my_y = lax.axis_index("gx"), lax.axis_index("gy")
-    others = []
-    for k in range(grid_y - 1):
-        high, low = grid_y - 1 - k, k
-        far_y = jnp.where(
-            my_y < grid_y // 2,
-            high - jnp.where(my_y >= high, 1, 0),
-            low + jnp.where(my_y <= low, 1, 0),
-        )
-        others += [(lax.rem(my_x + a, grid_x), far_y) for a in range(grid_x)]
-    others += [(lax.rem(my_x + a, grid_x), my_y) for a in range(1, grid_x)]
-
-    others = others[::-1]
+    rings = []
+    for k in range(1, grid_y):
+        step_y = jnp.where(my_y < grid_y // 2, k, grid_y - k)
+        rings.append(lax.rem(my_y + step_y, grid_y))
+    turns = [lax.rem(my_x + a, grid_x) for a in range(grid_x - 1, -1, -1)]
+    others = [(far_x, my_y) for far_x in turns[:-1]]
+    others += [(far_x, far_y) for far_x in turns for far_y in rings]
+
     barrier = pltpu.get_barrier_semaphore()
-    for offset in range(1, devices):
-        pl.semaphore_signal(barrier, inc=1, device_id=device_of(peer_at(offset)))
+    for far_x, far_y in others[::-1]:
+        pl.semaphore_signal(barrier, inc=1, device_id={"gx": far_x, "gy": far_y})
+    for load in loads:
+        load.start()
 
     lane_small = lax.broadcasted_iota(jnp.int32, (rows, lane_tile), 1)
 
@@ -168,25 +179,35 @@
     a_refs = (send_a, recv_a, a_send_sem, a_recv_sem, parts_a)
     b_refs = (send_b, recv_b, b_send_sem, b_recv_sem, parts_b)
 
-    def width_blocks(values, target):
-        for group in range(groups):
-            spec[...] = product(
-                jnp.concatenate(
-                    values[group * group_fields : (group + 1) * group_fields], axis=0
-                ),
-                fwd_y,
-            )
-            for d in range(devices):
-                tile, start = divmod(d * block, lane_tile)
-                tiles = [jnp.zeros((rows, lane_tile), f32)] * (padded // lane_tile)
-                for f in range(group_fields):
-                    to_tile, to_start = divmod(f * block, lane_tile)
-                    piece = spec[pl.ds(f * rows, rows), pl.ds(tile * lane_tile, lane_tile)]
-                    if to_start != start:
-                        piece = pltpu.roll(piece, (to_start - start) % lane_tile, 1)
-                    tiles[to_tile] = jnp.where(in_block(to_start), piece, tiles[to_tile])
-                for t, value in enumerate(tiles):
-                    target[group, d, :, pl.ds(t * lane_tile, lane_tile)] = value
+    slots = lane_tile // block
+    spread = freqs % 8 == 0
+    my_slot = lax.rem(me, slots)
+
+    def slot_of(turn, f):
+        return (turn + f) % slots if spread else f % slots
+
+    def width_blocks(values, target, parts, send):
+        spec[...] = product(jnp.concatenate(values, axis=0), fwd_y)
+        for n, part in enumerate(parts):
+            for j in range(devices // slots):
+                pieces = {}
+
+                def turned_piece(f, amount):
+                    if (f, amount) not in pieces:
+                        piece = spec[pl.ds(f * rows, rows), pl.ds(j * lane_tile, lane_tile)]
+                        pieces[f, amount] = pltpu.roll(piece, amount, 1) if amount else piece
+                    return pieces[f, amount]
+
+                for turn in range(slots):
+                    for t in range(*part):
+                        value = jnp.zeros((rows, lane_tile), f32)
+                        for k, f in enumerate(range(t * slots, min((t + 1) * slots, fields))):
+                            slot = slot_of(turn, f)
+                            piece = turned_piece(f, (slot - turn) % slots * block)
+                            full = k == 0 and fields - f >= slots
+                            value = piece if full else jnp.where(in_block(slot * block), piece, value)
+                        target[0, j * slots + turn, :, pl.ds(t * lane_tile, lane_tile)] = value
+            send(n)
 
     def mirrored(cells):
         values = [None] * fields
@@ -197,17 +218,20 @@
                 values[place(c, 1, z)] = a - b
         return values
 
-    def send_forward():
-        for n in range(len(parts_a)):
-            for o in others:
-                exchange(*a_refs, n, o).start()
-        recv_a[0, me] = send_a[0, me]
+    def send_forward(n):
+        for o in others:
+            exchange(*a_refs, n, o).start()
+        if n == len(parts_a) - 1:
+            recv_a[0, me] = send_a[0, me]
+
+    def send_first(n):
+        if n == 0:
+            pl.semaphore_wait(barrier, devices - 1)
+        send_forward(n)
 
     for load in loads[:2]:
         load.wait()
-    width_blocks(mirrored(magnet_ref), send_a)
-    pl.semaphore_wait(barrier, devices - 1)
-    send_forward()
+    width_blocks(mirrored(magnet_ref), send_a, parts_a, send_first)
     window_copy = pltpu.make_async_remote_copy(
         src_ref=magnet_ref, dst_ref=joined.at[:, pl.ds(rows, rows)],
         send_sem=win_sem.at[0], recv_sem=win_sem.at[1], device_id=device_of(left),
@@ -218,7 +242,7 @@
     fill_values = [
         jnp.full((rows, width), 2.0 if f // half == 5 else 0.0, f32) for f in range(fields)
     ]
-    width_blocks(fill_values, send_b)
+    width_blocks(fill_values, send_b, parts_b, lambda n: None)
     fill_ref[...] = send_b[:, me]
     for load in loads[2:]:
         load.wait()
@@ -282,42 +306,54 @@
                 exchange(*b_refs, n, o).start()
             recv_b[0, me, :, part] = send_b[0, me, :, part]
 
-        def hat(c, sign, z, odd):
-            first = place(c, sign, z) * block
+        def place_row(c, sign, z):
+            f = place(c, sign, z)
+            if not spread:
+                return f * block
+            return f // slots * lane_tile + lax.rem(my_slot + f % slots, slots) * block
+
+        def row_of(first, p, low):
+            row = first + p * freqs + low
+            return pl.multiple_of(row, 8) if spread else row
+
+        def hat(c, sign, z, odd, low, span):
+            first = place_row(c, sign, z)
             return tuple(
-                track_hat[pl.ds(first + p * freqs, freqs), pl.ds(odd * track, track)]
+                track_hat[pl.ds(row_of(first, p, low), span), pl.ds(odd * track, track)]
                 for p in range(2)
             )
 
         for chosen in range(2):
             if chosen < len(parts_a):
                 arrive(chosen)
-            for i in range(3):
-                sign = chosen ^ (i == 2)
-                for z in range(half):
-                    for odd in range(2):
-                        total = [None, None]
-                        for j in range(3):
-                            c = pair_comp[i][j]
-                            power = 1 if c >= 4 else 0
-                            swap = c in (3, 4)
-                            if swap:
-                                power += 1 if odd else 3
-                            for w in range(half):
-                                tab = table[c, z, w, sign, :, pl.ds(odd * track, track)]
-                                source = hat(
-                                    j, sign ^ (c >= 4), w, 1 - odd if swap else odd
-                                )
-                                parts = turned(power, tuple(tab * value for value in source))
-                                total = [
-                                    part if old is None else old + part
-                                    for old, part in zip(total, parts)
-                                ]
-                        first = place(i, sign, z) * block
-                        for p in range(2):
-                            track_prod[
-                                pl.ds(first + p * freqs, freqs), pl.ds(odd * track, track)
-                            ] = total[p]
+            span = min(freqs, 8)
+            for half_track in range(2):
+                for low in range(0, freqs, span):
+                    for i in range(3):
+                        odd = half_track if i == 0 else 1 - half_track
+                        columns = pl.ds(odd * track, track)
+                        sign = chosen ^ (i == 2)
+                        for z in range(half):
+                            total = [None, None]
+                            for j in range(3):
+                                c = pair_comp[i][j]
+                                power = 1 if c >= 4 else 0
+                                swap = c in (3, 4)
+                                if swap:
+                                    power += 1 if odd else 3
+                                for w in range(half):
+                                    tab = table[c, z, w, sign, pl.ds(low, span), columns]
+                                    source = hat(
+                                        j, sign ^ (c >= 4), w, 1 - odd if swap else odd, low, span
+                                    )
+                                    parts = turned(power, tuple(tab * value for value in source))
+                                    total = [
+                                        part if old is None else old + part
+                                        for old, part in zip(total, parts)
+                                    ]
+                            first = place_row(i, sign, z)
+                            for p in range(2):
+                                track_prod[pl.ds(row_of(first, p, low), span), columns] = total[p]
 
             if chosen == 1 or len(parts_b) == 2:
                 give_back(min(chosen, len(parts_b) - 1))
@@ -358,25 +394,32 @@
                 local_field[f] = effective
                 slope_ref[f] = drift * (0.5 * (down - up))
 
-        demag = []
-        for group in range(groups):
-            for f in range(group_fields):
-                from_tile, from_start = divmod(f * block, lane_tile)
-                for n, part in enumerate(parts_b):
-                    if from_start == 0 and from_tile == part[0]:
-                        all_blocks(*b_refs, n).wait_recv()
-                tiles = [None] * (2 * width // lane_tile)
-                for d in range(devices):
-                    tile, start = divmod(d * block, lane_tile)
-                    piece = recv_b[group, d, :, pl.ds(from_tile * lane_tile, lane_tile)]
-                    if from_start != start:
-                        piece = pltpu.roll(piece, (start - from_start) % lane_tile, 1)
-                    old = tiles[tile]
-                    tiles[tile] = piece if old is None else jnp.where(in_block(start), piece, old)
-                for t, value in enumerate(tiles):
-                    spec[pl.ds(f * rows, rows), pl.ds(t * lane_tile, lane_tile)] = value
-            field = product(spec[...], inv_y)
-            demag += [field[f * rows : (f + 1) * rows] for f in range(group_fields)]
+        for f in range(fields):
+            t = f // slots
+            for n, part in enumerate(parts_b):
+                if f == t * slots and t == part[0]:
+                    if n == len(parts_b) - 1:
+                        for refs in (a_refs, b_refs):
+                            for m in range(len(refs[-1])):
+                                all_blocks(*refs, m).wait_send()
+                    all_blocks(*b_refs, n).wait_recv()
+            for j in range(devices // slots):
+                value = None
+                for turn in range(slots):
+                    slot = slot_of(turn, f)
+                    piece = recv_b[0, j * slots + turn, :, pl.ds(t * lane_tile, lane_tile)]
+                    start = slot * block
+                    if not spread and slot != turn:
+                        piece = pltpu.roll(piece, (turn - slot) % slots * block, 1)
+                        start = turn * block
+                    elif not spread:
+                        start = turn * block
+                    value = piece if value is None else jnp.where(in_block(start), piece, value)
+                if spread and f % slots:
+                    value = pltpu.roll(value, (-f) % slots * block, 1)
+                spec[pl.ds(f * rows, rows), pl.ds(j * lane_tile, lane_tile)] = value
+        whole_field = product(spec[...], inv_y)
+        demag = [whole_field[f * rows : (f + 1) * rows] for f in range(fields)]
 
         weight = jnp.where((step == 0) | (step == 3), time_step / 6.0, time_step / 3.0)
         ahead = jnp.where(step == 2, time_step, 0.5 * time_step)
@@ -391,11 +434,7 @@
                 f = c * layers + z
                 even, odd = demag_of(c, 0, mirror), demag_of(c, 1, mirror)
                 value = local_field[f] + (even + odd if z < half else even - odd)
-
-                @pl.when(step == 0)
-                def _():
-                    field_ref[f] = value
-
+                local_field[f] = value
                 m.append(state[f])
                 h.append(value)
                 g.append(slope_ref[f])
@@ -421,19 +460,18 @@
                 next_ref[f] = next_ref[f] + weight * change
                 state[f] = initial[f] + ahead * change
 
-        for refs in (a_refs, b_refs):
-            for n in range(len(refs[-1])):
-                all_blocks(*refs, n).wait_send()
-
         @pl.when(step < 3)
         def _():
-            width_blocks(mirrored(state), send_a)
-            send_forward()
+            width_blocks(mirrored(state), send_a, parts_a, send_forward)
             for f in range(fields):
                 halo_out[0, pl.ds(f, 1), :] = state[f, pl.ds(0, 1), :]
                 halo_out[1, pl.ds(f, 1), :] = state[f, pl.ds(rows - 1, 1), :]
             for copy in halo_copies(step + 1):
                 copy.start()
+
+        @pl.when(step == 0)
+        def _():
+            field_ref[...] = local_field[...]
 
         return carry
 
@@ -454,13 +492,13 @@
     cells = (fields, rows, width)
     half = layers // 2
     blocks = (groups, devices, rows, padded)
-    out = pltpu.VMEM(cells, f32)
+    out = pltpu.VMEM((2, *cells), f32)
     dma = pltpu.SemaphoreType.DMA
-    magnet_next, field = pl.pallas_call(
+    both = pl.pallas_call(
         functools.partial(kernel_body, grid_y, devices, layers),
-        out_shape=(out, out),
+        out_shape=out,
         in_specs=[pl.BlockSpec(memory_space=pltpu.HBM)] * 8 + [pl.BlockSpec(memory_space=pltpu.SMEM)],
-        out_specs=(vmem, vmem),
+        out_specs=vmem,
         scratch_shapes=[
             pltpu.VMEM(cells, f32),
             pltpu.VMEM(tables[0].shape, bf16),
@@ -504,7 +542,7 @@
         region,
         window_shift,
     )
-    return magnet_next.reshape(magnet.shape), field.reshape(magnet.shape)
+    return both[0].reshape(magnet.shape), both[1].reshape(magnet.shape)
 
 
 def solution(mesh):

time: 64.5 us -> 62.5 us (0.969)
  Pallas kernels: 61.8 us -> 60.4 us
    pallas_call x1, Pallas kernels: 61.8 us -> 60.4 us  [local(): pl.pallas_call(functools.partial(kernel_body, grid_y, devices, layers), o...]
    unnamed x2 -> x0, local copies, waits for them, and re-layouts: 1.28 us -> none
    slice x0 -> x1, local copies, waits for them, and re-layouts: none -> 0.69 us  [local(): return (both[0].reshape(magnet.shape), both[1].reshape(magnet.shape))]
where the time goes in v2:
time: 62.5 us; the launch traced here: 62.3 us
  Pallas kernels  60.4 us (97%)
  between operations  1.28 us (2%)
  local copies, waits for them, and re-layouts  0.69 us (1%)
    pallas_call x1, Pallas kernels, local(): pl.pallas_call(functools.partial(kernel_body, grid_y, devices, layers), o...  60.4 us

profile of v2, /device:TPU:0, one launch (start us, length us, event | category | flops | bytes accessed | tf_op | source)
XLA Modules:
  0.0 62.3 jit_solution(18314733345728382868)
XLA Ops:
  1.3 60.4 %shard_map.104 = f32[2,12,8,256]{3,2,1,0:T(8,128)S(1)} custom-call(f32[12,8,256]{2,1,0:T(8,128)} %bitcast.3, bf16[256,1024]{1,0:T(8,128)(2,1)} %constant.8.clone.refs_1_, f32[6,7,16,256]{3,2,1,0:T(8,128)} %refs_2_.1, bf16[512,512]{1,0:T(8,128)(2,1)} %constant.9.clone.refs_3_, bf16[256,512]{1,0:T(8,128)(2,1)} %constant.10.clone.refs_4_, ...), custom_call_target="tpu_custom_call" | custom-call | tf_op jit(solution)/shard_map/pallas_call | solution.py:497
  61.7 0.7 %fusion = (f32[1,12,8,256]{3,2,1,0:T(8,128)}, f32[1,12,8,256]{3,2,1,0:T(8,128)}) fusion(f32[2,12,8,256]{3,2,1,0:T(8,128)S(1)} %shard_map.104), kind=kLoop, calls=%fused_computation | loop fusion | bytes 393216 | tf_op jit(solution)/shard_map/slice | solution.py:545

commit v3 on v2

--- a/solution.py
+++ b/solution.py
@@ -295,13 +295,17 @@
                 moved = jnp.where(cell >= beyond, fill_ref[0, pl.ds(0, 1), part], moved)
                 recv_a[0, :, :, part] = moved.reshape(devices, rows, part.size)
 
-            arrived = recv_a[0, :, :, part].reshape(track, part.size)
-            track_hat[part] = product(arrived.T, fwd_t)
+            for t in range(*parts_a[n]):
+                tile = pl.ds(t * lane_tile, lane_tile)
+                arrived = recv_a[0, :, :, tile].reshape(track, lane_tile)
+                track_hat[tile] = product(arrived.T, fwd_t)
 
         def give_back(n):
             part = lanes(parts_b[n])
-            back = product(track_prod[part], inv_t).T
-            send_b[0, :, :, part] = back.reshape(devices, rows, part.size)
+            for t in range(*parts_b[n]):
+                tile = pl.ds(t * lane_tile, lane_tile)
+                back = product(track_prod[tile], inv_t).T
+                send_b[0, :, :, tile] = back.reshape(devices, rows, lane_tile)
             for o in others:
                 exchange(*b_refs, n, o).start()
             recv_b[0, me, :, part] = send_b[0, me, :, part]

time: 62.5 us -> 62.2 us (level)
  no operation moved by 1% of the time
where the time goes in v3:
time: 62.2 us; the launch traced here: 62 us
  Pallas kernels  60 us (96%)
  between operations  1.28 us (2%)
  local copies, waits for them, and re-layouts  0.69 us (1%)
    pallas_call x1, Pallas kernels, local(): pl.pallas_call(functools.partial(kernel_body, grid_y, devices, layers), o...  60 us

profile of v3, /device:TPU:0, one launch (start us, length us, event | category | flops | bytes accessed | tf_op | source)
XLA Modules:
  0.0 62.0 jit_solution(7864939649316901429)
XLA Ops:
  1.3 60.0 %shard_map.104 = f32[2,12,8,256]{3,2,1,0:T(8,128)S(1)} custom-call(f32[12,8,256]{2,1,0:T(8,128)} %bitcast.3, bf16[256,1024]{1,0:T(8,128)(2,1)} %constant.8.clone.refs_1_, f32[6,7,16,256]{3,2,1,0:T(8,128)} %refs_2_.1, bf16[512,512]{1,0:T(8,128)(2,1)} %constant.9.clone.refs_3_, bf16[256,512]{1,0:T(8,128)(2,1)} %constant.10.clone.refs_4_, ...), custom_call_target="tpu_custom_call" | custom-call | tf_op jit(solution)/shard_map/pallas_call | solution.py:501
  61.3 0.7 %fusion = (f32[1,12,8,256]{3,2,1,0:T(8,128)}, f32[1,12,8,256]{3,2,1,0:T(8,128)}) fusion(f32[2,12,8,256]{3,2,1,0:T(8,128)S(1)} %shard_map.104), kind=kLoop, calls=%fused_computation | loop fusion | bytes 393216 | tf_op jit(solution)/shard_map/slice | solution.py:549
